TPU v7x, 32 devices: a whole 2x2x4 slice. The times are simulated.
32 devices in a mesh: depth: 4 (over z), imgx: 4 (over y, core), imgy: 2 (over x).
Axes of the slice: x: 2, y: 2, z: 4, core: 2. Of those that a mesh axis runs over, the one named last changes fastest.
Arguments:
- emissivity: bfloat16 [32, 512, 256], P('depth', 'imgx', 'imgy'), may hold values from 0.099609375 to 10
- bin_index: int32 [32, 512, 256], P('depth', 'imgx', 'imgy'), may hold values from 0 to 127
- color_table: bfloat16 [4, 128], replicated, may hold values from 0.049804688 to 1
- brick_order: int32 [4], replicated, may hold values from 0 to 3, each once
Outputs:
- image: float32 [4, 512, 256], P(None, 'imgx', 'imgy')
Inputs may be any that keep to these rules, and one draw needn't show every extreme that they name: brick_order names every brick index once.
All inputs are finite; a program needn't handle non-finite values.
Results may differ from a plain program's by a relative error of at most 0.0003.
Values sent between devices are 32-bit elements; how exact they have to be, the bound alone decides.
A program may use at most 64 MiB of HBM per device.

v0:
```python
import jax
import jax.numpy as jnp
from jax import lax
from jax.sharding import PartitionSpec as P


def on_device(emissivity, bin_index, color_table, brick_order):
    depth_cells, cols_x, cols_y = emissivity.shape
    pixels = cols_x * cols_y
    devices = lax.axis_size("depth")
    ray_step = 2.0 / (depth_cells * devices)
    levels = jnp.arange(color_table.shape[1], dtype=jnp.int32)

    def lookup(layer_bins):
        onehot = (layer_bins.reshape(1, pixels) == levels[:, None]).astype(jnp.bfloat16)
        return jnp.dot(color_table, onehot, preferred_element_type=jnp.float32)

    looked = lax.map(lookup, bin_index)
    bright = emissivity.reshape(depth_cells, pixels).astype(jnp.float32)
    glow_rgb = bright[:, None, :] * looked[:, 0:3, :]
    absorb_rate = bright * looked[:, 3, :]
    depth_in = jnp.cumsum(absorb_rate, axis=0) - absorb_rate
    light_in = jnp.exp(-ray_step * depth_in)
    color_sum = jnp.sum(ray_step * glow_rgb * light_in[:, None, :], axis=0)
    passed = jnp.exp(-ray_step * jnp.sum(absorb_rate, axis=0))
    piece_len = pixels // devices
    stacked = jnp.concatenate([color_sum, passed[None]], 0)[None]
    received = lax.all_to_all(stacked, "depth", split_axis=2, concat_axis=0, tiled=True)
    ordered = jnp.take(received, brick_order, axis=0)
    passed_all = ordered[:, 3, :]
    ahead_light = jnp.cumprod(
        jnp.concatenate([jnp.ones((1, piece_len), jnp.float32), passed_all[:-1]], 0), axis=0
    )
    my_color = jnp.sum(ordered[:, 0:3, :] * ahead_light[:, None, :], axis=0)
    through = jnp.prod(passed_all, axis=0)
    my_piece = jnp.concatenate([my_color, (1.0 - through)[None]], 0)
    full_tile = lax.all_gather(my_piece, "depth", axis=1, tiled=True)
    return full_tile.reshape(4, cols_x, cols_y)


def solution(mesh):
    return jax.shard_map(
        on_device,
        mesh=mesh,
        in_specs=(P("depth", "imgx", "imgy"), P("depth", "imgx", "imgy"), P(), P()),
        out_specs=P(None, "imgx", "imgy"),
        check_vma=False,
    )
```

profile of v0, /device:TPU:0, one launch (start us, length us, event | category | flops | bytes accessed | tf_op | source)
XLA Modules:
  0.0 172.7 jit_solution(10692280450666354)
XLA Ops:
  0.0 0.0 copy-start
  0.0 23.3 %while.11 = (s32[]{:T(128)}, f32[8,4,16384]{2,1,0:T(4,128)S(1)}, s32[8,128,128]{2,1,0:T(8,128)}, bf16[4,128]{1,0:T(4,128)(2,1)}, s32[]{:T(128)}) while((s32[]{:T(128)}, f32[8,4,16384]{2,1,0:T(4,128)S(1)}, s32[8,128,128]{2,1,0:T(8,128)}, bf16[4,128]{1,0:T(4,128)(2,1)}, s32[]{:T(128)}) %tuple.22), condition=%wide.region_1.2_spmd.clone, body=%wide.region_0.1_spmd.clone.sunk | while | flops 18874368 | bytes 459845 | solution.py:18
  0.0 0.9 dynamic-slice_bitcast_fusion.2
  0.9 2.1 %fusion.16 = f32[8,4,16384]{2,1,0:T(4,128)S(1)} fusion(f32[8,4,16384]{2,1,0:T(4,128)S(1)} %get-tuple-element.84, s32[]{:T(128)} %get-tuple-element.83, bf16[4,128]{1,0:T(4,128)(2,1)} %get-tuple-element.91, s32[16384]{0:T(1024)S(1)} %dynamic-slice_bitcast_fusion.2), kind=kOutput, calls=%fused_computation.3.clone.1 | convolution fusion | flops 18874368 | bytes 328708 | tf_op jit(solution)/shard_map/while/body/eval_jaxpr/dot_general | solution.py:16
  3.0 0.8 dynamic-slice_bitcast_fusion.2
  3.8 2.1 %fusion.16 = f32[8,4,16384]{2,1,0:T(4,128)S(1)} fusion(f32[8,4,16384]{2,1,0:T(4,128)S(1)} %get-tuple-element.84, s32[]{:T(128)} %get-tuple-element.83, bf16[4,128]{1,0:T(4,128)(2,1)} %get-tuple-element.91, s32[16384]{0:T(1024)S(1)} %dynamic-slice_bitcast_fusion.2), kind=kOutput, calls=%fused_computation.3.clone.1 | convolution fusion | flops 18874368 | bytes 328708 | tf_op jit(solution)/shard_map/while/body/eval_jaxpr/dot_general | solution.py:16
  5.9 0.8 dynamic-slice_bitcast_fusion.2
  6.7 2.1 %fusion.16 = f32[8,4,16384]{2,1,0:T(4,128)S(1)} fusion(f32[8,4,16384]{2,1,0:T(4,128)S(1)} %get-tuple-element.84, s32[]{:T(128)} %get-tuple-element.83, bf16[4,128]{1,0:T(4,128)(2,1)} %get-tuple-element.91, s32[16384]{0:T(1024)S(1)} %dynamic-slice_bitcast_fusion.2), kind=kOutput, calls=%fused_computation.3.clone.1 | convolution fusion | flops 18874368 | bytes 328708 | tf_op jit(solution)/shard_map/while/body/eval_jaxpr/dot_general | solution.py:16
  8.8 0.8 dynamic-slice_bitcast_fusion.2
  9.6 2.1 %fusion.16 = f32[8,4,16384]{2,1,0:T(4,128)S(1)} fusion(f32[8,4,16384]{2,1,0:T(4,128)S(1)} %get-tuple-element.84, s32[]{:T(128)} %get-tuple-element.83, bf16[4,128]{1,0:T(4,128)(2,1)} %get-tuple-element.91, s32[16384]{0:T(1024)S(1)} %dynamic-slice_bitcast_fusion.2), kind=kOutput, calls=%fused_computation.3.clone.1 | convolution fusion | flops 18874368 | bytes 328708 | tf_op jit(solution)/shard_map/while/body/eval_jaxpr/dot_general | solution.py:16
  11.7 0.8 dynamic-slice_bitcast_fusion.2
  12.5 2.1 %fusion.16 = f32[8,4,16384]{2,1,0:T(4,128)S(1)} fusion(f32[8,4,16384]{2,1,0:T(4,128)S(1)} %get-tuple-element.84, s32[]{:T(128)} %get-tuple-element.83, bf16[4,128]{1,0:T(4,128)(2,1)} %get-tuple-element.91, s32[16384]{0:T(1024)S(1)} %dynamic-slice_bitcast_fusion.2), kind=kOutput, calls=%fused_computation.3.clone.1 | convolution fusion | flops 18874368 | bytes 328708 | tf_op jit(solution)/shard_map/while/body/eval_jaxpr/dot_general | solution.py:16
  14.6 0.8 dynamic-slice_bitcast_fusion.2
  15.4 2.1 %fusion.16 = f32[8,4,16384]{2,1,0:T(4,128)S(1)} fusion(f32[8,4,16384]{2,1,0:T(4,128)S(1)} %get-tuple-element.84, s32[]{:T(128)} %get-tuple-element.83, bf16[4,128]{1,0:T(4,128)(2,1)} %get-tuple-element.91, s32[16384]{0:T(1024)S(1)} %dynamic-slice_bitcast_fusion.2), kind=kOutput, calls=%fused_computation.3.clone.1 | convolution fusion | flops 18874368 | bytes 328708 | tf_op jit(solution)/shard_map/while/body/eval_jaxpr/dot_general | solution.py:16
  17.5 0.8 dynamic-slice_bitcast_fusion.2
  18.3 2.1 %fusion.16 = f32[8,4,16384]{2,1,0:T(4,128)S(1)} fusion(f32[8,4,16384]{2,1,0:T(4,128)S(1)} %get-tuple-element.84, s32[]{:T(128)} %get-tuple-element.83, bf16[4,128]{1,0:T(4,128)(2,1)} %get-tuple-element.91, s32[16384]{0:T(1024)S(1)} %dynamic-slice_bitcast_fusion.2), kind=kOutput, calls=%fused_computation.3.clone.1 | convolution fusion | flops 18874368 | bytes 328708 | tf_op jit(solution)/shard_map/while/body/eval_jaxpr/dot_general | solution.py:16
  20.4 0.8 dynamic-slice_bitcast_fusion.2
  21.2 2.1 %fusion.16 = f32[8,4,16384]{2,1,0:T(4,128)S(1)} fusion(f32[8,4,16384]{2,1,0:T(4,128)S(1)} %get-tuple-element.84, s32[]{:T(128)} %get-tuple-element.83, bf16[4,128]{1,0:T(4,128)(2,1)} %get-tuple-element.91, s32[16384]{0:T(1024)S(1)} %dynamic-slice_bitcast_fusion.2), kind=kOutput, calls=%fused_computation.3.clone.1 | convolution fusion | flops 18874368 | bytes 328708 | tf_op jit(solution)/shard_map/while/body/eval_jaxpr/dot_general | solution.py:16
  23.3 0.0 copy-done
  23.3 0.1 fusion.11
  23.4 0.5 slice.18
  23.9 1.2 fusion.6
  25.2 0.3 copy.26
  25.5 0.3 copy.25
  25.8 0.7 fusion.7
  26.6 0.9 multiply_reduce_fusion
  27.5 0.1 pad_maximum_fusion
  27.6 5.1 %copy.8 = f32[4,16384]{0,1:T(8,128)} copy(f32[4,16384]{1,0:T(4,128)S(1)} %pad_maximum_fusion) | data formatting | bytes 524288 | tf_op jit(solution)/shard_map/concatenate | solution.py:27
  32.7 0.5 broadcast.39
  33.2 74.4 %reduce.1 = f32[16384,4]{1,0:T(8,128)} reduce(f32[16384,1,4]{2,1,0:T(1,128)} %bitcast.46, f32[]{:T(128)} %broadcast.39), dimensions={1}, to_apply=%bitcast.33.reduce_sub_computation | reduce | bytes 524292
  107.6 0.0 copy-start.1
  107.6 9.1 %reshape.72 = f32[4,1,16384]{2,1,0:T(1,128)} reshape(f32[16384,4]{1,0:T(8,128)} %reduce.1) | data formatting | bytes 524288
  116.7 6.3 %all-to-all-start = ((f32[4,1,16384]{2,1,0:T(1,128)}), f32[4,1,16384]{2,1,0:T(1,128)S(1)}, u32[]{:S(2)}, u32[]{:S(2)}) async-start(f32[4,1,16384]{2,1,0:T(1,128)} %reshape.72), calls=%async_computation | async-start | bytes 524288 | tf_op jit(solution)/shard_map/all_to_all | solution.py:28
  123.0 0.0 copy-done.1
  123.0 8.9 %all-to-all-done = f32[4,1,16384]{2,1,0:T(1,128)S(1)} async-done(((f32[4,1,16384]{2,1,0:T(1,128)}), f32[4,1,16384]{2,1,0:T(1,128)S(1)}, u32[]{:S(2)}, u32[]{:S(2)}) %all-to-all-start) | async-done | bytes 262176 | tf_op jit(solution)/shard_map/all_to_all | solution.py:28
  131.9 1.3 reduce.2
  133.2 17.7 %reshape.73 = f32[16384,1,4]{2,1,0:T(1,128)} reshape(f32[4,16384]{1,0:T(4,128)S(1)} %reduce.2) | data formatting | bytes 524288
  150.9 5.3 %copy.10 = f32[1,4,4,4096]{3,1,2,0:T(4,128)S(1)} copy(f32[1,4,4,4096]{1,3,2,0:T(8,128)} %bitcast.47) | data formatting | bytes 524288 | tf_op jit(solution)/shard_map/all_to_all | solution.py:28
  156.2 0.7 gather_fusion
  156.9 0.1 broadcast_select_fusion
  157.0 0.1 slice.25
  157.1 0.1 slice_reduce_fusion
  157.2 0.1 reduce_window.12
  157.3 0.1 fusion.9
  157.5 14.5 %all_gather.3 = f32[4,16384]{1,0:T(4,128)S(1)} all-gather(f32[4,4096]{1,0:T(4,128)S(1)} %pad_maximum_fusion.1), channel_id=1, replica_groups=mesh['depth'=4,'imgx'=4,'imgy'=2] {'depth'}, dimensions={1}, use_global_device_ids=true | all-gather | bytes 327680 | tf_op jit(solution)/shard_map/all_gather | solution.py:37
  171.9 0.7 copy.27
  (8 shorter events, 0.1 us)
Async XLA Ops:
  0.0 23.3 %copy-start = (bf16[8,128,128]{2,1,0:T(8,128)(2,1)S(1)}, bf16[8,128,128]{2,1,0:T(8,128)(2,1)}, u32[]{:S(2)}) copy-start(bf16[8,128,128]{2,1,0:T(8,128)(2,1)} %param.6) | copy-start | bytes 786436
  107.6 15.4 %copy-start.1 = (s32[4]{0:T(128)S(1)}, s32[4]{0:T(128)}, u32[]{:S(2)}) copy-start(s32[4]{0:T(128)} %param.9) | copy-start | bytes 52
  116.7 15.3 %all-to-all-start = ((f32[4,1,16384]{2,1,0:T(1,128)}), f32[4,1,16384]{2,1,0:T(1,128)S(1)}, u32[]{:S(2)}, u32[]{:S(2)}) async-start(f32[4,1,16384]{2,1,0:T(1,128)} %reshape.72), calls=%async_computation | async-start | bytes 524288 | tf_op jit(solution)/shard_map/all_to_all | solution.py:28
where the time goes:
time: 173 us
  other arithmetic  79.2 us (46%)
  local copies, waits for them, and re-layouts  47.1 us (27%)
  matrix products  16.5 us (10%)
  blocking collectives  14.5 us (8%)
  waiting for transfers between devices  8.87 us (5%)
  starting transfers between devices  6.35 us (4%)
    unnamed x1, other arithmetic  74.4 us
    unnamed x11, local copies, waits for them, and re-layouts  28.7 us
    dot_general x8, matrix products, lookup(): return jnp.dot(color_table, onehot, preferred_element_type=jnp.float32)  16.5 us
    all_gather x1, blocking collectives, on_device(): full_tile = lax.all_gather(my_piece, 'depth', axis=1, tiled=True)  14.5 us
    all_to_all x1, waiting for transfers between devices, on_device(): lax.all_to_all(stacked, 'depth', split_axis=2, concat_axis=0, tiled=True)  8.87 us
    eq x8, local copies, waits for them, and re-layouts, lookup(): layer_bins.reshape(1, pixels) == levels[:, None]  6.79 us
    all_to_all x1, starting transfers between devices, on_device(): lax.all_to_all(stacked, 'depth', split_axis=2, concat_axis=0, tiled=True)  6.35 us
    all_to_all x1, local copies, waits for them, and re-layouts, on_device(): lax.all_to_all(stacked, 'depth', split_axis=2, concat_axis=0, tiled=True)  5.3 us
  transfers between devices with their start and end apart: 1, of which 1 were waited for; matrix products, arithmetic and copies ran while one was open for 0% of the time, Pallas kernels for 0%

commit v1 on v0

--- a/solution.py
+++ b/solution.py
@@ -25,7 +25,12 @@
     passed = jnp.exp(-ray_step * jnp.sum(absorb_rate, axis=0))
     piece_len = pixels // devices
     stacked = jnp.concatenate([color_sum, passed[None]], 0)[None]
-    received = lax.all_to_all(stacked, "depth", split_axis=2, concat_axis=0, tiled=True)
+    received = jnp.concatenate(
+        lax.all_to_all(
+            jnp.stack(jnp.split(stacked, lax.axis_size("depth"), axis=2)), "depth", 0, 0
+        ),
+        axis=0,
+    )
     ordered = jnp.take(received, brick_order, axis=0)
     passed_all = ordered[:, 3, :]
     ahead_light = jnp.cumprod(

time: 173 us -> 60.8 us (0.35)
  other arithmetic: 79.2 us -> 4.31 us
  local copies, waits for them, and re-layouts: 47.1 us -> 9.49 us
    unnamed x1 -> x0, other arithmetic: 74.4 us -> none
    unnamed x11 -> x8, local copies, waits for them, and re-layouts: 28.7 us -> 1.39 us
    all_to_all x1 -> x0, local copies, waits for them, and re-layouts: 5.3 us -> none  [on_device(): lax.all_to_all(stacked, 'depth', split_axis=2, concat_axis=0, tiled=True)]
    concatenate x1 -> x0, local copies, waits for them, and re-layouts: 5.08 us -> none  [on_device(): stacked = jnp.concatenate([color_sum, passed[None]], 0)[None]]
where the time goes in v1:
time: 60.8 us; the launch traced here: 60.1 us
  matrix products  16.5 us (27%)
  blocking collectives  14.5 us (24%)
  local copies, waits for them, and re-layouts  9.49 us (16%)
  waiting for transfers between devices  8.87 us (15%)
  starting transfers between devices  6.35 us (10%)
  other arithmetic  4.31 us (7%)
    dot_general x8, matrix products, lookup(): return jnp.dot(color_table, onehot, preferred_element_type=jnp.float32)  16.5 us
    all_gather x1, blocking collectives, on_device(): full_tile = lax.all_gather(my_piece, 'depth', axis=1, tiled=True)  14.5 us
    all_to_all x1, waiting for transfers between devices, on_device(): lax.all_to_all(jnp.stack(jnp.split(stacked, lax.axis_size('depth'), axis=...  8.87 us
    eq x8, local copies, waits for them, and re-layouts, lookup(): layer_bins.reshape(1, pixels) == levels[:, None]  6.79 us
    all_to_all x1, starting transfers between devices, on_device(): lax.all_to_all(jnp.stack(jnp.split(stacked, lax.axis_size('depth'), axis=...  6.35 us
    unnamed x8, local copies, waits for them, and re-layouts  1.39 us
    another operation x1, other arithmetic, on_device(): depth_in = jnp.cumsum(absorb_rate, axis=0) - absorb_rate  1.24 us
  transfers between devices with their start and end apart: 1, of which 1 were waited for; matrix products, arithmetic and copies ran while one was open for 0% of the time, Pallas kernels for 0%

profile of v1, /device:TPU:0, one launch (start us, length us, event | category | flops | bytes accessed | tf_op | source)
XLA Modules:
  0.0 60.1 jit_solution(4742558048029132267)
XLA Ops:
  0.0 0.0 copy-start
  0.0 23.3 %while.11 = (s32[]{:T(128)}, f32[8,4,16384]{2,1,0:T(4,128)S(1)}, s32[8,128,128]{2,1,0:T(8,128)}, bf16[4,128]{1,0:T(4,128)(2,1)}, s32[]{:T(128)}) while((s32[]{:T(128)}, f32[8,4,16384]{2,1,0:T(4,128)S(1)}, s32[8,128,128]{2,1,0:T(8,128)}, bf16[4,128]{1,0:T(4,128)(2,1)}, s32[]{:T(128)}) %tuple.25), condition=%wide.region_1.2_spmd.clone, body=%wide.region_0.1_spmd.clone.sunk | while | flops 18874368 | bytes 459845 | solution.py:18
  0.0 0.9 %dynamic-slice_bitcast_fusion.2 = s32[16384]{0:T(1024)S(1)} fusion(s32[8,128,128]{2,1,0:T(8,128)} %get-tuple-element.94, s32[]{:T(128)} %get-tuple-element.87), kind=kLoop, calls=%fused_computation.6.clone.1 | loop fusion | bytes 131076 | tf_op jit(solution)/shard_map/while/body/eval_jaxpr/eq | solution.py:15
  0.9 2.1 %fusion.16 = f32[8,4,16384]{2,1,0:T(4,128)S(1)} fusion(f32[8,4,16384]{2,1,0:T(4,128)S(1)} %get-tuple-element.88, s32[]{:T(128)} %get-tuple-element.87, bf16[4,128]{1,0:T(4,128)(2,1)} %get-tuple-element.95, s32[16384]{0:T(1024)S(1)} %dynamic-slice_bitcast_fusion.2), kind=kOutput, calls=%fused_computation.3.clone.1 | convolution fusion | flops 18874368 | bytes 328708 | tf_op jit(solution)/shard_map/while/body/eval_jaxpr/dot_general | solution.py:16
  3.0 0.8 %dynamic-slice_bitcast_fusion.2 = s32[16384]{0:T(1024)S(1)} fusion(s32[8,128,128]{2,1,0:T(8,128)} %get-tuple-element.94, s32[]{:T(128)} %get-tuple-element.87), kind=kLoop, calls=%fused_computation.6.clone.1 | loop fusion | bytes 131076 | tf_op jit(solution)/shard_map/while/body/eval_jaxpr/eq | solution.py:15
  3.8 2.1 %fusion.16 = f32[8,4,16384]{2,1,0:T(4,128)S(1)} fusion(f32[8,4,16384]{2,1,0:T(4,128)S(1)} %get-tuple-element.88, s32[]{:T(128)} %get-tuple-element.87, bf16[4,128]{1,0:T(4,128)(2,1)} %get-tuple-element.95, s32[16384]{0:T(1024)S(1)} %dynamic-slice_bitcast_fusion.2), kind=kOutput, calls=%fused_computation.3.clone.1 | convolution fusion | flops 18874368 | bytes 328708 | tf_op jit(solution)/shard_map/while/body/eval_jaxpr/dot_general | solution.py:16
  5.9 0.8 %dynamic-slice_bitcast_fusion.2 = s32[16384]{0:T(1024)S(1)} fusion(s32[8,128,128]{2,1,0:T(8,128)} %get-tuple-element.94, s32[]{:T(128)} %get-tuple-element.87), kind=kLoop, calls=%fused_computation.6.clone.1 | loop fusion | bytes 131076 | tf_op jit(solution)/shard_map/while/body/eval_jaxpr/eq | solution.py:15
  6.7 2.1 %fusion.16 = f32[8,4,16384]{2,1,0:T(4,128)S(1)} fusion(f32[8,4,16384]{2,1,0:T(4,128)S(1)} %get-tuple-element.88, s32[]{:T(128)} %get-tuple-element.87, bf16[4,128]{1,0:T(4,128)(2,1)} %get-tuple-element.95, s32[16384]{0:T(1024)S(1)} %dynamic-slice_bitcast_fusion.2), kind=kOutput, calls=%fused_computation.3.clone.1 | convolution fusion | flops 18874368 | bytes 328708 | tf_op jit(solution)/shard_map/while/body/eval_jaxpr/dot_general | solution.py:16
  8.8 0.8 %dynamic-slice_bitcast_fusion.2 = s32[16384]{0:T(1024)S(1)} fusion(s32[8,128,128]{2,1,0:T(8,128)} %get-tuple-element.94, s32[]{:T(128)} %get-tuple-element.87), kind=kLoop, calls=%fused_computation.6.clone.1 | loop fusion | bytes 131076 | tf_op jit(solution)/shard_map/while/body/eval_jaxpr/eq | solution.py:15
  9.6 2.1 %fusion.16 = f32[8,4,16384]{2,1,0:T(4,128)S(1)} fusion(f32[8,4,16384]{2,1,0:T(4,128)S(1)} %get-tuple-element.88, s32[]{:T(128)} %get-tuple-element.87, bf16[4,128]{1,0:T(4,128)(2,1)} %get-tuple-element.95, s32[16384]{0:T(1024)S(1)} %dynamic-slice_bitcast_fusion.2), kind=kOutput, calls=%fused_computation.3.clone.1 | convolution fusion | flops 18874368 | bytes 328708 | tf_op jit(solution)/shard_map/while/body/eval_jaxpr/dot_general | solution.py:16
  11.7 0.8 %dynamic-slice_bitcast_fusion.2 = s32[16384]{0:T(1024)S(1)} fusion(s32[8,128,128]{2,1,0:T(8,128)} %get-tuple-element.94, s32[]{:T(128)} %get-tuple-element.87), kind=kLoop, calls=%fused_computation.6.clone.1 | loop fusion | bytes 131076 | tf_op jit(solution)/shard_map/while/body/eval_jaxpr/eq | solution.py:15
  12.5 2.1 %fusion.16 = f32[8,4,16384]{2,1,0:T(4,128)S(1)} fusion(f32[8,4,16384]{2,1,0:T(4,128)S(1)} %get-tuple-element.88, s32[]{:T(128)} %get-tuple-element.87, bf16[4,128]{1,0:T(4,128)(2,1)} %get-tuple-element.95, s32[16384]{0:T(1024)S(1)} %dynamic-slice_bitcast_fusion.2), kind=kOutput, calls=%fused_computation.3.clone.1 | convolution fusion | flops 18874368 | bytes 328708 | tf_op jit(solution)/shard_map/while/body/eval_jaxpr/dot_general | solution.py:16
  14.6 0.8 %dynamic-slice_bitcast_fusion.2 = s32[16384]{0:T(1024)S(1)} fusion(s32[8,128,128]{2,1,0:T(8,128)} %get-tuple-element.94, s32[]{:T(128)} %get-tuple-element.87), kind=kLoop, calls=%fused_computation.6.clone.1 | loop fusion | bytes 131076 | tf_op jit(solution)/shard_map/while/body/eval_jaxpr/eq | solution.py:15
  15.4 2.1 %fusion.16 = f32[8,4,16384]{2,1,0:T(4,128)S(1)} fusion(f32[8,4,16384]{2,1,0:T(4,128)S(1)} %get-tuple-element.88, s32[]{:T(128)} %get-tuple-element.87, bf16[4,128]{1,0:T(4,128)(2,1)} %get-tuple-element.95, s32[16384]{0:T(1024)S(1)} %dynamic-slice_bitcast_fusion.2), kind=kOutput, calls=%fused_computation.3.clone.1 | convolution fusion | flops 18874368 | bytes 328708 | tf_op jit(solution)/shard_map/while/body/eval_jaxpr/dot_general | solution.py:16
  17.5 0.8 %dynamic-slice_bitcast_fusion.2 = s32[16384]{0:T(1024)S(1)} fusion(s32[8,128,128]{2,1,0:T(8,128)} %get-tuple-element.94, s32[]{:T(128)} %get-tuple-element.87), kind=kLoop, calls=%fused_computation.6.clone.1 | loop fusion | bytes 131076 | tf_op jit(solution)/shard_map/while/body/eval_jaxpr/eq | solution.py:15
  18.3 2.1 %fusion.16 = f32[8,4,16384]{2,1,0:T(4,128)S(1)} fusion(f32[8,4,16384]{2,1,0:T(4,128)S(1)} %get-tuple-element.88, s32[]{:T(128)} %get-tuple-element.87, bf16[4,128]{1,0:T(4,128)(2,1)} %get-tuple-element.95, s32[16384]{0:T(1024)S(1)} %dynamic-slice_bitcast_fusion.2), kind=kOutput, calls=%fused_computation.3.clone.1 | convolution fusion | flops 18874368 | bytes 328708 | tf_op jit(solution)/shard_map/while/body/eval_jaxpr/dot_general | solution.py:16
  20.4 0.8 %dynamic-slice_bitcast_fusion.2 = s32[16384]{0:T(1024)S(1)} fusion(s32[8,128,128]{2,1,0:T(8,128)} %get-tuple-element.94, s32[]{:T(128)} %get-tuple-element.87), kind=kLoop, calls=%fused_computation.6.clone.1 | loop fusion | bytes 131076 | tf_op jit(solution)/shard_map/while/body/eval_jaxpr/eq | solution.py:15
  21.2 2.1 %fusion.16 = f32[8,4,16384]{2,1,0:T(4,128)S(1)} fusion(f32[8,4,16384]{2,1,0:T(4,128)S(1)} %get-tuple-element.88, s32[]{:T(128)} %get-tuple-element.87, bf16[4,128]{1,0:T(4,128)(2,1)} %get-tuple-element.95, s32[16384]{0:T(1024)S(1)} %dynamic-slice_bitcast_fusion.2), kind=kOutput, calls=%fused_computation.3.clone.1 | convolution fusion | flops 18874368 | bytes 328708 | tf_op jit(solution)/shard_map/while/body/eval_jaxpr/dot_general | solution.py:16
  23.3 0.0 copy-done
  23.3 0.1 fusion.11
  23.4 0.5 slice.18
  23.9 1.2 %fusion.6 = f32[8,1,16384]{2,1,0:T(1,128)S(1)} fusion(f32[8,1,16384]{2,1,0:T(1,128)S(1)} %bitcast.50, f32[8,4,16384]{2,1,0:T(4,128)S(1)} %get-tuple-element.32), kind=kOutput, calls=%fused_computation.10 | output fusion | flops 1441792 | bytes 1572864 | tf_op jit(solution)/shard_map/jit(cumsum)/reduce_window_sum | solution.py:22
  25.2 0.3 copy.27
  25.5 0.3 copy.26
  25.8 0.7 %fusion.7 = f32[16384]{0:T(1024)S(1)} fusion(f32[8,1,16384]{2,1,0:T(1,128)S(1)} %slice.18, f32[1,8,128,128]{3,2,1,0:T(8,128)S(1)} %get-tuple-element.56), kind=kLoop, calls=%fused_computation.14 | loop fusion | flops 245760 | bytes 1114112 | tf_op jit(solution)/shard_map/reduce_sum | solution.py:25
  26.6 0.0 copy-start.1
  26.6 0.9 %multiply_reduce_fusion = f32[3,16384]{1,0:T(4,128)S(1)} fusion(f32[8,4,16384]{2,1,0:T(4,128)S(1)} %get-tuple-element.32, f32[8,16384]{1,0:T(8,128)S(1)} %bitcast.51, f32[8,16384]{1,0:T(8,128)S(1)} %bitcast.52), kind=kLoop, calls=%fused_computation.11 | loop fusion | flops 1130496 | bytes 2818048 | tf_op jit(solution)/shard_map/reduce_sum | solution.py:24
  27.5 0.1 maximum_bitcast_fusion
  27.6 0.8 %pad_maximum_fusion = f32[4,1,4,4096]{3,2,1,0:T(4,128)} fusion(f32[1,1,4,4096]{3,2,1,0:T(4,128)S(1)} %get-tuple-element.52, f32[1,1,4,4096]{3,2,1,0:T(4,128)S(1)} %get-tuple-element.53, f32[1,1,4,4096]{3,2,1,0:T(4,128)S(1)} %get-tuple-element.54, f32[1,1,4,4096]{3,2,1,0:T(4,128)S(1)} %get-tuple-element.51), kind=kLoop, calls=%fused_computation.21 | loop fusion | flops 196608 | bytes 524288 | tf_op jit(solution)/shard_map/stack | solution.py:30
  28.4 6.3 %all-to-all-start = ((f32[4,1,4,4096]{3,2,1,0:T(4,128)}), f32[4,1,4,4096]{3,2,1,0:T(4,128)S(1)}, u32[]{:S(2)}, u32[]{:S(2)}) async-start(f32[4,1,4,4096]{3,2,1,0:T(4,128)} %pad_maximum_fusion), calls=%async_computation | async-start | bytes 524288 | tf_op jit(solution)/shard_map/all_to_all | solution.py:29
  34.8 0.0 copy-done.1
  34.8 8.9 %all-to-all-done = f32[4,1,4,4096]{3,2,1,0:T(4,128)S(1)} async-done(((f32[4,1,4,4096]{3,2,1,0:T(4,128)}), f32[4,1,4,4096]{3,2,1,0:T(4,128)S(1)}, u32[]{:S(2)}, u32[]{:S(2)}) %all-to-all-start) | async-done | bytes 262176 | tf_op jit(solution)/shard_map/all_to_all | solution.py:29
  43.7 0.7 %gather_fusion = f32[4,4,4096]{2,1,0:T(4,128)S(1)} fusion(f32[4,4,4096]{2,1,0:T(4,128)S(1)} %bitcast.53, s32[1024]{0:T(1024)S(1)} %pad_clamp_fusion), kind=kCustom, calls=%fused_computation | custom fusion | bytes 524304 | tf_op jit(solution)/shard_map/jit(_take)/gather | solution.py:34
  44.4 0.1 broadcast_select_fusion
  44.5 0.1 slice.25
  44.6 0.1 slice_reduce_fusion
  44.7 0.1 reduce_window.12
  44.8 0.1 fusion.9
  44.9 14.5 %all_gather.3 = f32[4,16384]{1,0:T(4,128)S(1)} all-gather(f32[4,4096]{1,0:T(4,128)S(1)} %pad_maximum_fusion.1), channel_id=1, replica_groups=mesh['depth'=4,'imgx'=4,'imgy'=2] {'depth'}, dimensions={1}, use_global_device_ids=true | all-gather | bytes 327680 | tf_op jit(solution)/shard_map/all_gather | solution.py:42
  59.4 0.7 %copy.28 = f32[1,4,128,128]{3,2,1,0:T(8,128)} copy(f32[1,4,128,128]{3,1,2,0:T(4,128)S(1)} %bitcast.54) | data formatting | bytes 524288
  (9 shorter events, 0.1 us)
Async XLA Ops:
  0.0 23.3 %copy-start = (bf16[8,128,128]{2,1,0:T(8,128)(2,1)S(1)}, bf16[8,128,128]{2,1,0:T(8,128)(2,1)}, u32[]{:S(2)}) copy-start(bf16[8,128,128]{2,1,0:T(8,128)(2,1)} %param.6) | copy-start | bytes 786436
  26.6 8.2 %copy-start.1 = (s32[4]{0:T(128)S(1)}, s32[4]{0:T(128)}, u32[]{:S(2)}) copy-start(s32[4]{0:T(128)} %param.9) | copy-start | bytes 52
  28.4 15.3 %all-to-all-start = ((f32[4,1,4,4096]{3,2,1,0:T(4,128)}), f32[4,1,4,4096]{3,2,1,0:T(4,128)S(1)}, u32[]{:S(2)}, u32[]{:S(2)}) async-start(f32[4,1,4,4096]{3,2,1,0:T(4,128)} %pad_maximum_fusion), calls=%async_computation | async-start | bytes 524288 | tf_op jit(solution)/shard_map/all_to_all | solution.py:29
